TPU v7x, 768 devices: a whole 4x8x12 slice. The times are simulated.
768 devices in a mesh: ta: 16 (over y, x_lo), gz: 4 (over x_hi, core), xy: 12 (over z).
Axes of the slice: x: 4 (x_hi: 2, x_lo: 2; x = x_hi * 2 + x_lo), y: 8, z: 12, core: 2. Of those that a mesh axis runs over, the one named last changes fastest.
Arguments:
- source_field: float32 [2, 4, 3, 16, 4, 12, 128], P(None, None, None, 'ta', 'gz', 'xy'), may hold values from -6 to 6
- gauge_links: float32 [2, 8, 3, 3, 16, 4, 12, 128], P(None, None, None, None, 'ta', 'gz', 'xy'), may hold values from -2.5 to 2.5
- fine_vectors: bfloat16 [2, 24, 4, 3, 16, 4, 12, 128], P(None, None, None, None, 'ta', 'gz', 'xy'), may hold values from -1.75 to 1.75
- middle_blocks: float32 [2, 9, 24, 16, 4, 12, 768], P(None, None, None, 'ta', 'gz', 'xy'), may hold values from -0.3125 to 0.3125
- middle_vectors: float32 [2, 24, 16, 4, 12, 768], P(None, None, 'ta', 'gz', 'xy'), may hold values from -0.625 to 0.625
- bottom_blocks: float32 [2, 7, 16, 4, 6912], P(None, None, 'ta', 'gz'), may hold values from -4 to 4
Outputs:
- solution: float32 [2, 4, 3, 16, 4, 12, 128], P(None, None, None, 'ta', 'gz', 'xy')
- smoothed_residual: float32 [2, 4, 3, 16, 4, 12, 128], P(None, None, None, 'ta', 'gz', 'xy')
All inputs are finite; a program needn't handle non-finite values.
Results may differ from a plain program's by a relative error of at most 0.0034.
Values sent between devices are 32-bit elements; how exact they have to be, the bound alone decides.
A program may use at most 64 MiB of HBM per device.

v0:
```python
import functools

import jax
import jax.numpy as jnp
import numpy as np
from jax import lax
from jax.experimental import pallas as pl
from jax.experimental.pallas import tpu as pltpu
from jax.sharding import PartitionSpec as P

MESH = pl.DeviceIdType.MESH
F32 = jnp.float32
BF16 = jnp.bfloat16

DIAGONAL = 4.1
TWIST = 0.1
DENOMINATOR = DIAGONAL * DIAGONAL + TWIST * TWIST
PRE_SAME = 0.8 * DIAGONAL / DENOMINATOR
PRE_OTHER = 0.8 * TWIST / DENOMINATOR

STEPS = ((1, 0, 0), (-1, 0, 0), (0, 1, 0), (0, -1, 0), (0, 0, 1), (0, 0, -1))
NEAR = ((0, 0, 0),) + STEPS


def added(one, other):
    return tuple(a + b for a, b in zip(one, other))


def plan(sizes):
    def wrapped(offset):
        return tuple(o % n for o, n in zip(offset, sizes))

    slots = {}
    for one in NEAR:
        for other in NEAR:
            slots.setdefault(wrapped(added(one, other)), len(slots))
    plane = {}
    for dt in range(sizes[0]):
        for dz in range(sizes[1]):
            plane[(dt, dz, 0)] = len(plane)
    line = {(0, 0, dx): dx for dx in range(sizes[2])}
    peers = set(slots) | set(plane) | set(line)
    peers.discard((0, 0, 0))
    return wrapped, slots, plane, line, sorted(peers)


def tables():
    lane = np.arange(128)
    spread = np.zeros((128, 1280), np.float32)
    collect = np.zeros((640, 128), np.float32)
    for j in range(24):
        for k in range(24):
            spread[k, j * 24 + k] = 1
            spread[32 + k, 640 + j * 24 + k] = 1
            collect[j * 24 + k, j] = 1
    unfold = (lane[:, None] % 32 == lane[None] // 4).astype(np.float32)
    share = (lane[:, None] // 4 == lane[None] // 4).astype(np.float32)
    square = np.concatenate([unfold, unfold.T, share], 0)
    return spread, collect, square


def pieces(value):
    high = value.astype(BF16)
    rest = value - high.astype(F32)
    middle = rest.astype(BF16)
    low = (rest - middle.astype(F32)).astype(BF16)
    return high, middle, low


def times_table(value, table):
    high, middle, low = pieces(value)
    return (
        jnp.dot(high, table, preferred_element_type=F32)
        + jnp.dot(middle, table, preferred_element_type=F32)
        + jnp.dot(low, table, preferred_element_type=F32)
    )


def row_sums(value):
    ones = jnp.ones((8, 128), BF16)
    dims = (((1,), (1,)), ((), ()))
    return sum(
        lax.dot_general(ones, piece, dims, preferred_element_type=F32) for piece in pieces(value)
    )


def kernel(
    sizes,
    src_h, gauge_h, fine_h, mblk_h, mvec_h, bblk_h, spread_h, collect_h, square_h,
    sol_ref, res_ref,
    src, gauge, fine, mblk, mvec, bblk, spread, collect, square,
    halo, hop_rows, second, fine_f, mv_parts, own_blk, got_blk, near_blk,
    right_rows, sum_rows, around, spread_rows, gram_rows, plane_rows, line_rows, mid, wide, final,
    local_sem, halo_send, halo_recv, blk_send, blk_recv, right_send, right_recv,
    plane_send, plane_recv, line_send, line_recv, mid_send, mid_recv,
):
    wrapped, slots, plane, line, peers = plan(sizes)
    here = tuple(lax.axis_index(axis) for axis in ("ta", "gz", "xy"))

    def at(offset):
        return tuple(
            h if o % n == 0 else lax.rem(h + (o % n), n) for h, o, n in zip(here, offset, sizes)
        )

    def against(offset):
        return at(tuple(-o for o in offset))

    loads = [
        pltpu.make_async_copy(a, b, local_sem.at[i])
        for i, (a, b) in enumerate(
            (
                (src_h, src), (gauge_h, gauge), (bblk_h, bblk), (fine_h, fine), (mvec_h, mvec),
                (spread_h, spread), (collect_h, collect), (square_h, square), (mblk_h, mblk),
            )
        )
    ]
    for load in loads:
        load.start()

    barrier = pltpu.get_barrier_semaphore()
    for offset in peers:
        pl.semaphore_signal(barrier, inc=1, device_id=at(offset), device_id_type=MESH)

    def remote(source, target, send, recv, device):
        return pltpu.make_async_remote_copy(
            src_ref=source, dst_ref=target, send_sem=send, recv_sem=recv,
            device_id=device, device_id_type=MESH,
        )

    def halo_copies(source, which):
        return [
            remote(
                source, halo.at[which, d], halo_send.at[which, d], halo_recv.at[which, d],
                against(STEPS[d]),
            )
            for d in range(6)
        ]

    loads[0].wait()
    pl.semaphore_wait(barrier, len(peers))
    first_copies = halo_copies(src, 0)
    for copy in first_copies:
        copy.start()

    lanes8 = lax.broadcasted_iota(jnp.int32, (8, 128), 1)
    low_half = lanes8 < 64
    near_blk[...] = jnp.zeros_like(near_blk)
    own_blk[...] = jnp.zeros_like(own_blk)
    around[...] = jnp.zeros_like(around)
    sum_rows[...] = jnp.zeros_like(sum_rows)
    gram_rows[...] = jnp.zeros_like(gram_rows)
    mv_parts[...] = jnp.zeros_like(mv_parts)
    loads[2].wait()
    per_x = bblk.shape[0] // 14

    def site_blocks(x):
        start = (x * 9) // 2
        odd = lax.rem(x, 2) == 1
        for p in range(2):
            chunks = [
                bblk[pl.ds(p * 7 * per_x + start + q, 7, stride=per_x), 0, :] for q in range(5)
            ]
            for q in range(5):
                here_now = chunks[q]
                after = chunks[min(q + 1, 4)]
                moved = jnp.where(
                    low_half[:7], pltpu.roll(here_now, 64, 1), pltpu.roll(after, 64, 1)
                )
                yield p, q, jnp.where(odd, moved, here_now)

    for p, q, value in site_blocks(here[2]):
        own_blk[p, q, pl.ds(0, 7), :] = value
        near_blk[p, q, pl.ds(0, 7, stride=8), :] = value
    blk_copies = [
        remote(own_blk, got_blk.at[d], blk_send.at[d], blk_recv.at[d], against(STEPS[d]))
        for d in range(4)
    ]
    for copy in blk_copies:
        copy.start()
    for d in (4, 5):
        for p, q, value in site_blocks(at(STEPS[d])[2]):
            near_blk[p, q, pl.ds(1 + d, 7, stride=8), :] = value
    loads[3].wait()
    fine_f[...] = fine[...].astype(F32)
    loads[4].wait()
    for p in range(2):
        for c in range(6):
            block = mvec[pl.ds(p * 144 + c, 24, stride=6), :]
            high = block.astype(BF16)
            mv_parts[p, 0, pl.ds(0, 24), pl.ds(c * 128, 128)] = high
            mv_parts[p, 1, pl.ds(0, 24), pl.ds(c * 128, 128)] = (block - high.astype(F32)).astype(BF16)

    direction = lax.broadcasted_iota(jnp.int32, (8, 128), 0)
    is_t = direction < 2
    is_z = direction < 4
    is_x = direction < 6
    odd_one = lax.rem(direction, 2) == 1
    base = jnp.where(odd_one, 1.0, -1.0).astype(F32)
    in_z = jnp.logical_and(is_z, jnp.logical_not(is_t))
    in_x = jnp.logical_and(is_x, jnp.logical_not(is_z))
    in_y = jnp.logical_not(is_x)

    def flipped(mask):
        return jnp.where(mask, -base, base)

    sign_a = flipped(jnp.logical_not(is_t))
    sign_b = flipped(in_y)
    sign_c = flipped(in_x)
    sign_d = flipped(in_z)
    sign_e = flipped(jnp.logical_or(in_z, in_x))
    sign_f = flipped(jnp.logical_or(in_z, in_y))
    sign_g = flipped(jnp.logical_or(in_x, in_y))

    def pick(a, b, c, d):
        return jnp.where(is_t, a, jnp.where(is_z, b, jnp.where(is_x, c, d)))

    loads[1].wait()

    def hopping(near):
        link = [
            [[gauge[pl.ds(p * 72 + c * 3 + e, 8, stride=9), :] for e in range(3)] for c in range(3)]
            for p in range(2)
        ]
        (r0, r1, r2, r3), (i0, i1, i2, i3) = near
        half = [[[None] * 3 for _ in range(2)] for _ in range(2)]
        for c in range(3):
            half[0][0][c] = r0[c] + sign_a * pick(r2[c], i2[c], i3[c], r3[c])
            half[1][0][c] = i0[c] + sign_b * pick(i2[c], r2[c], r3[c], i3[c])
            half[0][1][c] = r1[c] + sign_c * pick(r3[c], i3[c], i2[c], r2[c])
            half[1][1][c] = i1[c] + sign_d * pick(i3[c], r3[c], r2[c], i2[c])

        def put(p, s, c, value):
            hop_rows[pl.ds(p * 12 + s * 3 + c, 1), :] = jnp.sum(value, axis=0, keepdims=True)

        for c in range(3):
            moved = [[0.0, 0.0], [0.0, 0.0]]
            for s in range(2):
                for e in range(3):
                    lr, li = link[0][c][e], link[1][c][e]
                    hr, hi = half[0][s][e], half[1][s][e]
                    moved[0][s] = moved[0][s] + (lr * hr - li * hi)
                    moved[1][s] = moved[1][s] + (lr * hi + li * hr)
            (a0, a1), (b0, b1) = moved
            put(0, 0, c, a0)
            put(0, 1, c, a1)
            put(1, 0, c, b0)
            put(1, 1, c, b1)
            put(0, 2, c, base * pick(a0, b0, b1, a1))
            put(1, 2, c, sign_e * pick(b0, a0, a1, b1))
            put(0, 3, c, sign_f * pick(a1, b1, b0, a0))
            put(1, 3, c, sign_g * pick(b1, a1, a0, b0))

    def near_values(which):
        return [
            [
                [halo[which, :, p * 12 + s * 3 + c, :] for c in range(3)]
                for s in range(4)
            ]
            for p in range(2)
        ]

    def fill_y(which, field):
        halo[which, 6] = pltpu.roll(field, 127, 1)
        halo[which, 7] = pltpu.roll(field, 1, 1)

    rows12 = lax.broadcasted_iota(jnp.int32, (12, 128), 0)
    chiral = jnp.where(rows12 < 6, 1.0, -1.0).astype(F32)

    def smoothed(re, im):
        return (
            PRE_SAME * re + PRE_OTHER * (chiral * im),
            PRE_SAME * im - PRE_OTHER * (chiral * re),
        )

    def residual(re, im):
        hop_re, hop_im = hop_rows[0:12, :], hop_rows[12:24, :]
        out_re = src[0:12, :] - (DIAGONAL * re - TWIST * (chiral * im) - 0.5 * hop_re)
        out_im = src[12:24, :] - (DIAGONAL * im + TWIST * (chiral * re) - 0.5 * hop_im)
        return out_re, out_im

    fill_y(0, src[...])
    for copy in first_copies:
        copy.wait_recv()
    raw = near_values(0)
    ready = [[[None] * 3 for _ in range(4)] for _ in range(2)]
    for s in range(4):
        other = PRE_OTHER if s < 2 else -PRE_OTHER
        for c in range(3):
            re, im = raw[0][s][c], raw[1][s][c]
            ready[0][s][c] = PRE_SAME * re + other * im
            ready[1][s][c] = PRE_SAME * im - other * re
    hopping(ready)
    first_re, first_im = smoothed(src[0:12, :], src[12:24, :])
    left_re, left_im = smoothed(*residual(first_re, first_im))
    second_re, second_im = first_re + left_re, first_im + left_im
    second[0:12, :] = second_re
    second[12:24, :] = second_im
    second_copies = halo_copies(second, 1)
    for copy in second_copies:
        copy.start()

    for d in range(4):
        blk_copies[d].wait_recv()
        for p in range(2):
            for q in range(5):
                near_blk[p, q, pl.ds(1 + d, 7, stride=8), :] = got_blk[d, p, q, pl.ds(0, 7), :]
    for load in loads[5:8]:
        load.wait()

    fill_y(1, second[...])
    for copy in second_copies:
        copy.wait_recv()
    hopping(near_values(1))
    res_re, res_im = residual(second_re, second_im)
    res_ref[0:12, :] = res_re
    res_ref[12:24, :] = res_im
    hop_rows[0:12, :] = res_re.astype(BF16).astype(F32)
    hop_rows[12:24, :] = res_im.astype(BF16).astype(F32)

    def fine_vector(p, s, c):
        return fine_f[pl.ds(p * 288 + c * 4 + s, 24, stride=12), :]

    part_re = jnp.zeros((24, 128), F32)
    part_im = jnp.zeros((24, 128), F32)
    for s in range(4):
        for c in range(3):
            vr, vi = fine_vector(0, s, c), fine_vector(1, s, c)
            rr = hop_rows[pl.ds(s * 3 + c, 1), :]
            ri = hop_rows[pl.ds(12 + s * 3 + c, 1), :]
            part_re = part_re + (vr * rr + vi * ri)
            part_im = part_im + (vr * ri - vi * rr)
    parts = jnp.concatenate([part_re, part_im], axis=0)
    wide[0:48, :] = times_table(parts, square[128:256, :])
    lane_row = lax.broadcasted_iota(jnp.int32, (1, 128), 1)

    def middle_row(p, c):
        rows = [wide[pl.ds(p * 24 + c * 4 + g, 1), :] for g in range(4)]
        return jnp.where(
            lane_row < 64,
            jnp.where(lane_row < 32, rows[0], rows[1]),
            jnp.where(lane_row < 96, rows[2], rows[3]),
        )

    q_re = jnp.zeros((24, 128), F32)
    q_im = jnp.zeros((24, 128), F32)
    for c in range(6):
        vr = mvec[pl.ds(c, 24, stride=6), :]
        vi = mvec[pl.ds(144 + c, 24, stride=6), :]
        mr, mi = middle_row(0, c), middle_row(1, c)
        q_re = q_re + (vr * mr + vi * mi)
        q_im = q_im + (vr * mi - vi * mr)
    sum_rows[0:24, :] = q_re
    sum_rows[32:56, :] = q_im
    right_rows[pl.ds(0, 1)] = row_sums(sum_rows[...])[0:1].reshape(1, 1, 128)

    right_copies = [
        remote(
            right_rows.at[0], right_rows.at[slot], right_send.at[slot], right_recv.at[slot],
            against(offset),
        )
        for offset, slot in slots.items()
        if slot
    ]
    for copy in right_copies:
        copy.start()
    final[pl.ds(96, 48), :] = 0.4 * times_table(parts, square[256:384, :])
    for copy in right_copies:
        copy.wait_recv()

    for d in range(7):
        for i in range(7):
            slot = slots[wrapped(added(NEAR[d], NEAR[i]))]
            around[pl.ds(d * 8 + i, 1), :] = right_rows[slot]
    spread_rows[...] = times_table(around[...], spread[...])
    image_re, image_im = [], []
    for q in range(5):
        sum_re = jnp.zeros((8, 128), F32)
        sum_im = jnp.zeros((8, 128), F32)
        for d in range(7):
            br = near_blk[0, q, pl.ds(d * 8, 8), :]
            bi = near_blk[1, q, pl.ds(d * 8, 8), :]
            xr = spread_rows[pl.ds(d * 8, 8), pl.ds(q * 128, 128)]
            xi = spread_rows[pl.ds(d * 8, 8), pl.ds(640 + q * 128, 128)]
            sum_re = sum_re + (br * xr - bi * xi)
            sum_im = sum_im + (br * xi + bi * xr)
        image_re.append(sum_re)
        image_im.append(sum_im)
    image = jnp.concatenate(
        [jnp.concatenate(image_re, axis=1), jnp.concatenate(image_im, axis=1)], axis=0
    )
    image = times_table(image, collect[...])
    inside = lanes8 < 24
    rows_now = around[0:8, :]
    right_re = jnp.where(inside, rows_now, 0.0)
    right_im = jnp.where(inside, pltpu.roll(rows_now, 96, 1), 0.0)
    one_re = 2.0 * right_re + image[0:8]
    one_im = 2.0 * right_im + image[8:16]

    ahead = times_table(jnp.concatenate([one_re, one_im], axis=0), spread[:, 0:640])
    image_re, image_im = [], []
    for q in range(5):
        br, bi = own_blk[0, q], own_blk[1, q]
        xr = ahead[0:8, q * 128:(q + 1) * 128]
        xi = ahead[8:16, q * 128:(q + 1) * 128]
        image_re.append(br * xr - bi * xi)
        image_im.append(br * xi + bi * xr)
    image = jnp.concatenate(
        [jnp.concatenate(image_re, axis=1), jnp.concatenate(image_im, axis=1)], axis=0
    )
    image = times_table(image, collect[...])
    fr, fi = one_re[0:1], one_im[0:1]
    sr = 2.0 * fr + jnp.sum(image[0:8], axis=0, keepdims=True)
    si = 2.0 * fi + jnp.sum(image[8:16], axis=0, keepdims=True)
    rr, ri = right_re[0:1], right_im[0:1]
    products = (
        fr * fr + fi * fi,
        sr * sr + si * si,
        fr * sr + fi * si,
        fr * si - fi * sr,
        fr * rr + fi * ri,
        fr * ri - fi * rr,
        sr * rr + si * ri,
        sr * ri - si * rr,
    )
    for i, value in enumerate(products):
        gram_rows[pl.ds(i, 1), :] = value
    plane_rows[pl.ds(0, 1)] = row_sums(gram_rows[...])[0:1].reshape(1, 1, 128)
    plane_copies = [
        remote(plane_rows.at[0], plane_rows.at[slot], plane_send, plane_recv, against(offset))
        for offset, slot in plane.items()
        if slot
    ]
    for copy in plane_copies:
        copy.start()

    left = jnp.concatenate([rr, ri, fr, fi], axis=0)
    turned = jnp.concatenate([-ri, rr, -fi, fr], axis=0)
    guess = jnp.zeros((4, 768), F32)
    for p, rows in ((0, left), (1, turned)):
        high = rows.astype(BF16)
        low = (rows - high.astype(F32)).astype(BF16)
        guess = guess + jnp.dot(high[:, 0:32], mv_parts[p, 0], preferred_element_type=F32)
        guess = guess + jnp.dot(low[:, 0:32], mv_parts[p, 0], preferred_element_type=F32)
        guess = guess + jnp.dot(high[:, 0:32], mv_parts[p, 1], preferred_element_type=F32)
    mid[0] = guess
    mid_copies = [
        remote(mid.at[0], mid.at[1 + d], mid_send.at[d], mid_recv.at[d], against(STEPS[d]))
        for d in range(6)
    ]
    for copy in mid_copies:
        copy.start()
    lanes4 = lax.broadcasted_iota(jnp.int32, (4, 128), 1)
    place4 = lax.rem(lanes4, 32)
    for c in range(6):
        now = guess[:, c * 128:(c + 1) * 128]
        mid[7, :, pl.ds(c * 128, 128)] = jnp.where(
            place4 == 31, pltpu.roll(now, 31, 1), pltpu.roll(now, 127, 1)
        )
        mid[8, :, pl.ds(c * 128, 128)] = jnp.where(
            place4 == 0, pltpu.roll(now, 97, 1), pltpu.roll(now, 1, 1)
        )
    loads[8].wait()

    def middle_step(d, sums):
        sums = list(sums)
        for c in range(6):
            br = mblk[pl.ds(d * 144 + c, 24, stride=6), :]
            bi = mblk[pl.ds((9 + d) * 144 + c, 24, stride=6), :]
            for v in range(2):
                xr = mid[d, pl.ds(2 * v, 1), pl.ds(c * 128, 128)]
                xi = mid[d, pl.ds(2 * v + 1, 1), pl.ds(c * 128, 128)]
                sums[2 * v] = sums[2 * v] + (br * xr - bi * xi)
                sums[2 * v + 1] = sums[2 * v + 1] + (br * xi + bi * xr)
        return tuple(sums)

    sums = tuple(jnp.zeros((24, 128), F32) for _ in range(4))
    sums = middle_step(0, sums)
    sums = lax.fori_loop(7, 9, middle_step, sums)

    count = len(plane)
    every = plane_rows.at[pl.ds(1, count - 1)]
    remote(every, every, plane_send, plane_recv, here).wait_recv()
    together = jnp.sum(plane_rows[...].reshape(count, 128), axis=0, keepdims=True)
    line_rows[pl.ds(0, 1)] = together.reshape(1, 1, 128)
    line_copies = [
        remote(line_rows.at[0], line_rows.at[slot], line_send, line_recv, against(offset))
        for offset, slot in line.items()
        if slot
    ]
    for copy in line_copies:
        copy.start()

    for copy in mid_copies:
        copy.wait_recv()
    sums = lax.fori_loop(1, 7, middle_step, sums)
    rows24 = lax.broadcasted_iota(jnp.int32, (24, 128), 0)
    lanes24 = lax.broadcasted_iota(jnp.int32, (24, 128), 1)
    mine = lax.rem(rows24, 4) == lanes24 // 32
    for i in range(4):
        for c in range(6):
            wide[pl.ds(i * 24 + c * 4, 4), :] = jnp.broadcast_to(
                mid[0, pl.ds(i, 1), pl.ds(c * 128, 128)], (4, 128)
            )
    changes = [
        0.2 * jnp.where(mine, wide[pl.ds(i * 24, 24), :], 0.0) - 0.4 * sums[i] for i in range(4)
    ]
    final[pl.ds(0, 96), :] = times_table(jnp.concatenate(changes, axis=0), square[0:128, :])

    count = len(line)
    every = line_rows.at[pl.ds(1, count - 1)]
    remote(every, every, line_send, line_recv, here).wait_recv()
    totals = jnp.sum(line_rows[...].reshape(count, 128), axis=0, keepdims=True)
    first_norm, second_norm, cross_re, cross_im, ar, ai, br, bi = (
        jnp.broadcast_to(totals[:, i:i + 1], (1, 128)) for i in range(8)
    )
    determinant = first_norm * second_norm - cross_re * cross_re - cross_im * cross_im
    one_r = (second_norm * ar - (cross_re * br - cross_im * bi)) / determinant
    one_i = (second_norm * ai - (cross_re * bi + cross_im * br)) / determinant
    two_r = (first_norm * br - (cross_re * ar + cross_im * ai)) / determinant
    two_i = (first_norm * bi - (cross_re * ai - cross_im * ar)) / determinant
    ur, ui, wr, wi = (final[pl.ds(i * 24, 24), :] for i in range(4))
    update_re = final[96:120, :] + (one_r * ur - one_i * ui) + (two_r * wr - two_i * wi)
    update_im = final[120:144, :] + (one_r * ui + one_i * ur) + (two_r * wi + two_i * wr)
    update_re = update_re.astype(BF16).astype(F32)
    update_im = update_im.astype(BF16).astype(F32)
    for s in range(4):
        for c in range(3):
            vr, vi = fine_vector(0, s, c), fine_vector(1, s, c)
            add_re = jnp.sum(vr * update_re - vi * update_im, axis=0, keepdims=True)
            add_im = jnp.sum(vr * update_im + vi * update_re, axis=0, keepdims=True)
            row = s * 3 + c
            sol_ref[pl.ds(row, 1), :] = second[pl.ds(row, 1), :] + add_re
            sol_ref[pl.ds(12 + row, 1), :] = second[pl.ds(12 + row, 1), :] + add_im

    for copy in first_copies + second_copies + blk_copies + right_copies + mid_copies:
        copy.wait_send()
    every = plane_rows.at[pl.ds(1, len(plane) - 1)]
    remote(every, every, plane_send, plane_recv, here).wait_send()
    every = line_rows.at[pl.ds(1, len(line) - 1)]
    remote(every, every, line_send, line_recv, here).wait_send()


def solution(mesh):
    sizes = tuple(mesh.shape[axis] for axis in ("ta", "gz", "xy"))
    slots = plan(sizes)[1]

    def shards(source_field, gauge_links, fine_vectors, middle_blocks, middle_vectors, bottom_blocks):
        spread, collect, square = (jnp.asarray(t, BF16) for t in tables())
        fine = jnp.transpose(fine_vectors, (0, 1, 3, 4, 5, 6, 2, 7)).reshape(576, 128)
        operands = (
            source_field.reshape(24, 128),
            gauge_links.reshape(144, 128),
            fine,
            middle_blocks.reshape(2592, 128),
            middle_vectors.reshape(288, 128),
            bottom_blocks.reshape(-1, 1, 128),
            spread,
            collect,
            square,
        )
        vmem = [pltpu.VMEM(o.shape, o.dtype) for o in operands]
        dma = pltpu.SemaphoreType.DMA
        sol, res = pl.pallas_call(
            functools.partial(kernel, sizes),
            out_shape=(jax.ShapeDtypeStruct((24, 128), F32),) * 2,
            in_specs=[pl.BlockSpec(memory_space=pltpu.HBM)] * len(operands),
            out_specs=(pl.BlockSpec(memory_space=pltpu.VMEM),) * 2,
            scratch_shapes=vmem
            + [
                pltpu.VMEM((2, 8, 24, 128), F32),
                pltpu.VMEM((24, 128), F32),
                pltpu.VMEM((24, 128), F32),
                pltpu.VMEM((576, 128), F32),
                pltpu.VMEM((2, 2, 32, 768), BF16),
                pltpu.VMEM((2, 5, 8, 128), F32),
                pltpu.VMEM((4, 2, 5, 8, 128), F32),
                pltpu.VMEM((2, 5, 56, 128), F32),
                pltpu.VMEM((len(slots), 1, 128), F32),
                pltpu.VMEM((128, 128), F32),
                pltpu.VMEM((56, 128), F32),
                pltpu.VMEM((56, 1280), F32),
                pltpu.VMEM((128, 128), F32),
                pltpu.VMEM((sizes[0] * sizes[1], 1, 128), F32),
                pltpu.VMEM((sizes[2], 1, 128), F32),
                pltpu.VMEM((9, 4, 768), F32),
                pltpu.VMEM((96, 128), F32),
                pltpu.VMEM((144, 128), F32),
                dma((len(operands),)),
                dma((2, 6)),
                dma((2, 6)),
                dma((4,)),
                dma((4,)),
                dma((len(slots),)),
                dma((len(slots),)),
                dma,
                dma,
                dma,
                dma,
                dma((6,)),
                dma((6,)),
            ],
            compiler_params=pltpu.CompilerParams(collective_id=0, has_side_effects=True),
        )(*operands)
        return sol.reshape(source_field.shape), res.reshape(source_field.shape)

    return jax.shard_map(
        shards,
        mesh=mesh,
        in_specs=(
            P(None, None, None, "ta", "gz", "xy", None),
            P(None, None, None, None, "ta", "gz", "xy", None),
            P(None, None, None, None, "ta", "gz", "xy", None),
            P(None, None, None, "ta", "gz", "xy", None),
            P(None, None, "ta", "gz", "xy", None),
            P(None, None, "ta", "gz", None),
        ),
        out_specs=(
            P(None, None, None, "ta", "gz", "xy", None),
            P(None, None, None, "ta", "gz", "xy", None),
        ),
        check_vma=False,
    )
```

profile of v0, /device:TPU:1, one launch (start us, length us, event | category | flops | bytes accessed | tf_op | source)
XLA Modules:
  0.0 50.1 jit_solution(999575170519775705)
XLA Ops:
  0.6 46.8 %shard_map.104 = (f32[24,128]{1,0:T(8,128)}, f32[24,128]{1,0:T(8,128)}) custom-call(f32[24,128]{1,0:T(8,128)} %bitcast.15, f32[144,128]{1,0:T(8,128)} %bitcast.14, bf16[576,128]{1,0:T(8,128)(2,1)} %bitcast.12, f32[2592,128]{1,0:T(8,128)} %bitcast.10, f32[288,128]{1,0:T(8,128)} %bitcast.13, f32[756,1,128]{2,1,0:T(1,128)} %bitcast.11, ...), custom_call_target="tpu_custom_call" | custom-call | tf_op jit(solution)/shard_map/pallas_call | solution.py:563
  47.4 1.3 %copy.17 = f32[2,4,3,1,1,1,128]{6,5,4,3,2,1,0:T(1,128)} copy(f32[2,4,3,1,1,1,128]{6,5,4,3,2,1,0:T(1,128)} %bitcast.17) | data formatting | bytes 24576
  48.8 1.3 %copy.18 = f32[2,4,3,1,1,1,128]{6,5,4,3,2,1,0:T(1,128)} copy(f32[2,4,3,1,1,1,128]{6,5,4,3,2,1,0:T(1,128)} %bitcast.16) | data formatting | bytes 24576
where the time goes:
time: 50.4 us; the launch traced here: 50.1 us
  Pallas kernels  46.8 us (93%)
  local copies, waits for them, and re-layouts  2.62 us (5%)
  between operations  0.64 us (1%)
    pallas_call x1, Pallas kernels, shards(): pl.pallas_call(functools.partial(kernel, sizes), out_shape=(jax.ShapeDtyp...  46.8 us
    unnamed x2, local copies, waits for them, and re-layouts  2.62 us

commit v1 on v0

--- a/solution.py
+++ b/solution.py
@@ -39,9 +39,7 @@
         for dz in range(sizes[1]):
             plane[(dt, dz, 0)] = len(plane)
     line = {(0, 0, dx): dx for dx in range(sizes[2])}
-    peers = set(slots) | set(plane) | set(line)
-    peers.discard((0, 0, 0))
-    return wrapped, slots, plane, line, sorted(peers)
+    return wrapped, slots, plane, line
 
 
 def tables():
@@ -92,9 +90,9 @@
     halo, hop_rows, second, fine_f, mv_parts, own_blk, got_blk, near_blk,
     right_rows, sum_rows, around, spread_rows, gram_rows, plane_rows, line_rows, mid, wide, final,
     local_sem, halo_send, halo_recv, blk_send, blk_recv, right_send, right_recv,
-    plane_send, plane_recv, line_send, line_recv, mid_send, mid_recv,
+    plane_send, plane_recv, line_send, line_recv, mid_send, mid_recv, near_token, far_token,
 ):
-    wrapped, slots, plane, line, peers = plan(sizes)
+    wrapped, slots, plane, line = plan(sizes)
     here = tuple(lax.axis_index(axis) for axis in ("ta", "gz", "xy"))
 
     def at(offset):
@@ -118,8 +116,8 @@
         load.start()
 
     barrier = pltpu.get_barrier_semaphore()
-    for offset in peers:
-        pl.semaphore_signal(barrier, inc=1, device_id=at(offset), device_id_type=MESH)
+    for step in STEPS:
+        pl.semaphore_signal(barrier, inc=1, device_id=at(step), device_id_type=MESH)
 
     def remote(source, target, send, recv, device):
         return pltpu.make_async_remote_copy(
@@ -127,20 +125,37 @@
             device_id=device, device_id_type=MESH,
         )
 
-    def halo_copies(source, which):
-        return [
-            remote(
-                source, halo.at[which, d], halo_send.at[which, d], halo_recv.at[which, d],
-                against(STEPS[d]),
-            )
-            for d in range(6)
-        ]
+    class Group:
+        def __init__(self, source, target, send, recv, places):
+            self.all = [
+                remote(source, target.at[slot], send, recv, against(offset)) for offset, slot in places
+            ]
+            low = min(slot for _, slot in places)
+            whole = target.at[pl.ds(low, len(places))]
+            self.sum = remote(whole, whole, send, recv, here)
+
+        def start(self):
+            for copy in self.all:
+                copy.start()
+            return self
+
+        def arrived(self):
+            self.sum.wait_recv()
+
+        def sent(self):
+            self.sum.wait_send()
+
+    def greet(offsets, token):
+        far = [offset for offset in offsets if any(wrapped(offset))]
+        for offset in far:
+            pl.semaphore_signal(token, inc=1, device_id=at(offset), device_id_type=MESH)
+        return len(far)
+
+    six = [(STEPS[d], d) for d in range(6)]
 
     loads[0].wait()
-    pl.semaphore_wait(barrier, len(peers))
-    first_copies = halo_copies(src, 0)
-    for copy in first_copies:
-        copy.start()
+    pl.semaphore_wait(barrier, len(STEPS))
+    first_copies = Group(src, halo.at[0], halo_send.at[0], halo_recv.at[0], six).start()
 
     lanes8 = lax.broadcasted_iota(jnp.int32, (8, 128), 1)
     low_half = lanes8 < 64
@@ -171,12 +186,6 @@
     for p, q, value in site_blocks(here[2]):
         own_blk[p, q, pl.ds(0, 7), :] = value
         near_blk[p, q, pl.ds(0, 7, stride=8), :] = value
-    blk_copies = [
-        remote(own_blk, got_blk.at[d], blk_send.at[d], blk_recv.at[d], against(STEPS[d]))
-        for d in range(4)
-    ]
-    for copy in blk_copies:
-        copy.start()
     for d in (4, 5):
         for p, q, value in site_blocks(at(STEPS[d])[2]):
             near_blk[p, q, pl.ds(1 + d, 7, stride=8), :] = value
@@ -279,8 +288,8 @@
         return out_re, out_im
 
     fill_y(0, src[...])
-    for copy in first_copies:
-        copy.wait_recv()
+    first_copies.arrived()
+    near_count = greet([(2, 0, 0), (-2, 0, 0), (0, 0, 2), (0, 0, -2)], near_token)
     raw = near_values(0)
     ready = [[[None] * 3 for _ in range(4)] for _ in range(2)]
     for s in range(4):
@@ -295,21 +304,13 @@
     second_re, second_im = first_re + left_re, first_im + left_im
     second[0:12, :] = second_re
     second[12:24, :] = second_im
-    second_copies = halo_copies(second, 1)
-    for copy in second_copies:
-        copy.start()
-
-    for d in range(4):
-        blk_copies[d].wait_recv()
-        for p in range(2):
-            for q in range(5):
-                near_blk[p, q, pl.ds(1 + d, 7, stride=8), :] = got_blk[d, p, q, pl.ds(0, 7), :]
+    second_copies = Group(second, halo.at[1], halo_send.at[1], halo_recv.at[1], six).start()
+    blk_copies = Group(own_blk, got_blk, blk_send, blk_recv, six[:4]).start()
     for load in loads[5:8]:
         load.wait()
 
     fill_y(1, second[...])
-    for copy in second_copies:
-        copy.wait_recv()
+    second_copies.arrived()
     hopping(near_values(1))
     res_re, res_im = residual(second_re, second_im)
     res_ref[0:12, :] = res_re
@@ -353,19 +354,19 @@
     sum_rows[32:56, :] = q_im
     right_rows[pl.ds(0, 1)] = row_sums(sum_rows[...])[0:1].reshape(1, 1, 128)
 
-    right_copies = [
-        remote(
-            right_rows.at[0], right_rows.at[slot], right_send.at[slot], right_recv.at[slot],
-            against(offset),
-        )
-        for offset, slot in slots.items()
-        if slot
-    ]
-    for copy in right_copies:
-        copy.start()
+    if near_count:
+        pl.semaphore_wait(near_token, near_count)
+    right_copies = Group(
+        right_rows.at[0], right_rows, right_send, right_recv, [o for o in slots.items() if o[1]]
+    ).start()
     final[pl.ds(96, 48), :] = 0.4 * times_table(parts, square[256:384, :])
-    for copy in right_copies:
-        copy.wait_recv()
+    blk_copies.arrived()
+    for d in range(4):
+        for p in range(2):
+            for q in range(5):
+                near_blk[p, q, pl.ds(1 + d, 7, stride=8), :] = got_blk[d, p, q, pl.ds(0, 7), :]
+    right_copies.arrived()
+    far_count = greet([(4, 0, 0), (-4, 0, 0)], far_token)
 
     for d in range(7):
         for i in range(7):
@@ -424,14 +425,10 @@
     )
     for i, value in enumerate(products):
         gram_rows[pl.ds(i, 1), :] = value
-    plane_rows[pl.ds(0, 1)] = row_sums(gram_rows[...])[0:1].reshape(1, 1, 128)
-    plane_copies = [
-        remote(plane_rows.at[0], plane_rows.at[slot], plane_send, plane_recv, against(offset))
-        for offset, slot in plane.items()
-        if slot
-    ]
-    for copy in plane_copies:
-        copy.start()
+    line_rows[pl.ds(0, 1)] = row_sums(gram_rows[...])[0:1].reshape(1, 1, 128)
+    line_copies = Group(
+        line_rows.at[0], line_rows, line_send, line_recv, [o for o in line.items() if o[1]]
+    ).start()
 
     left = jnp.concatenate([rr, ri, fr, fi], axis=0)
     turned = jnp.concatenate([-ri, rr, -fi, fr], axis=0)
@@ -443,12 +440,9 @@
         guess = guess + jnp.dot(low[:, 0:32], mv_parts[p, 0], preferred_element_type=F32)
         guess = guess + jnp.dot(high[:, 0:32], mv_parts[p, 1], preferred_element_type=F32)
     mid[0] = guess
-    mid_copies = [
-        remote(mid.at[0], mid.at[1 + d], mid_send.at[d], mid_recv.at[d], against(STEPS[d]))
-        for d in range(6)
-    ]
-    for copy in mid_copies:
-        copy.start()
+    mid_copies = Group(
+        mid.at[0], mid, mid_send, mid_recv, [(STEPS[d], 1 + d) for d in range(6)]
+    ).start()
     lanes4 = lax.broadcasted_iota(jnp.int32, (4, 128), 1)
     place4 = lax.rem(lanes4, 32)
     for c in range(6):
@@ -477,21 +471,16 @@
     sums = middle_step(0, sums)
     sums = lax.fori_loop(7, 9, middle_step, sums)
 
-    count = len(plane)
-    every = plane_rows.at[pl.ds(1, count - 1)]
-    remote(every, every, plane_send, plane_recv, here).wait_recv()
-    together = jnp.sum(plane_rows[...].reshape(count, 128), axis=0, keepdims=True)
-    line_rows[pl.ds(0, 1)] = together.reshape(1, 1, 128)
-    line_copies = [
-        remote(line_rows.at[0], line_rows.at[slot], line_send, line_recv, against(offset))
-        for offset, slot in line.items()
-        if slot
-    ]
-    for copy in line_copies:
-        copy.start()
-
-    for copy in mid_copies:
-        copy.wait_recv()
+    line_copies.arrived()
+    together = jnp.sum(line_rows[...].reshape(len(line), 128), axis=0, keepdims=True)
+    plane_rows[pl.ds(0, 1)] = together.reshape(1, 1, 128)
+    if far_count:
+        pl.semaphore_wait(far_token, far_count)
+    plane_copies = Group(
+        plane_rows.at[0], plane_rows, plane_send, plane_recv, [o for o in plane.items() if o[1]]
+    ).start()
+
+    mid_copies.arrived()
     sums = lax.fori_loop(1, 7, middle_step, sums)
     rows24 = lax.broadcasted_iota(jnp.int32, (24, 128), 0)
     lanes24 = lax.broadcasted_iota(jnp.int32, (24, 128), 1)
@@ -506,10 +495,8 @@
     ]
     final[pl.ds(0, 96), :] = times_table(jnp.concatenate(changes, axis=0), square[0:128, :])
 
-    count = len(line)
-    every = line_rows.at[pl.ds(1, count - 1)]
-    remote(every, every, line_send, line_recv, here).wait_recv()
-    totals = jnp.sum(line_rows[...].reshape(count, 128), axis=0, keepdims=True)
+    plane_copies.arrived()
+    totals = jnp.sum(plane_rows[...].reshape(len(plane), 128), axis=0, keepdims=True)
     first_norm, second_norm, cross_re, cross_im, ar, ai, br, bi = (
         jnp.broadcast_to(totals[:, i:i + 1], (1, 128)) for i in range(8)
     )
@@ -532,12 +519,21 @@
             sol_ref[pl.ds(row, 1), :] = second[pl.ds(row, 1), :] + add_re
             sol_ref[pl.ds(12 + row, 1), :] = second[pl.ds(12 + row, 1), :] + add_im
 
-    for copy in first_copies + second_copies + blk_copies + right_copies + mid_copies:
-        copy.wait_send()
-    every = plane_rows.at[pl.ds(1, len(plane) - 1)]
-    remote(every, every, plane_send, plane_recv, here).wait_send()
-    every = line_rows.at[pl.ds(1, len(line) - 1)]
-    remote(every, every, line_send, line_recv, here).wait_send()
+    for group in (
+        first_copies, second_copies, blk_copies, right_copies, line_copies, mid_copies, plane_copies
+    ):
+        group.sent()
+
+
+def deliver(sol_v, res_v, sol_h, res_h, sem):
+    copies = (
+        pltpu.make_async_copy(sol_v, sol_h, sem.at[0]),
+        pltpu.make_async_copy(res_v, res_h, sem.at[1]),
+    )
+    for copy in copies:
+        copy.start()
+    for copy in copies:
+        copy.wait()
 
 
 def solution(mesh):
@@ -562,7 +558,7 @@
         dma = pltpu.SemaphoreType.DMA
         sol, res = pl.pallas_call(
             functools.partial(kernel, sizes),
-            out_shape=(jax.ShapeDtypeStruct((24, 128), F32),) * 2,
+            out_shape=(pltpu.VMEM((24, 128), F32),) * 2,
             in_specs=[pl.BlockSpec(memory_space=pltpu.HBM)] * len(operands),
             out_specs=(pl.BlockSpec(memory_space=pltpu.VMEM),) * 2,
             scratch_shapes=vmem
@@ -586,21 +582,20 @@
                 pltpu.VMEM((96, 128), F32),
                 pltpu.VMEM((144, 128), F32),
                 dma((len(operands),)),
-                dma((2, 6)),
-                dma((2, 6)),
-                dma((4,)),
-                dma((4,)),
-                dma((len(slots),)),
-                dma((len(slots),)),
-                dma,
-                dma,
-                dma,
-                dma,
-                dma((6,)),
-                dma((6,)),
-            ],
+                dma((2,)),
+                dma((2,)),
+            ]
+            + [dma] * 10
+            + [pltpu.SemaphoreType.REGULAR] * 2,
             compiler_params=pltpu.CompilerParams(collective_id=0, has_side_effects=True),
         )(*operands)
+        sol, res = pl.pallas_call(
+            deliver,
+            out_shape=(jax.ShapeDtypeStruct((24, 128), F32),) * 2,
+            in_specs=[pl.BlockSpec(memory_space=pltpu.VMEM)] * 2,
+            out_specs=(pl.BlockSpec(memory_space=pltpu.HBM),) * 2,
+            scratch_shapes=[pltpu.SemaphoreType.DMA((2,))],
+        )(*(pltpu.with_memory_space_constraint(o, pltpu.VMEM) for o in (sol, res)))
         return sol.reshape(source_field.shape), res.reshape(source_field.shape)
 
     return jax.shard_map(

time: 50.4 us -> 44.9 us (0.89)
  Pallas kernels: 46.8 us -> 44.1 us
  local copies, waits for them, and re-layouts: 2.62 us -> 0 us
    pallas_call x1 -> x2, Pallas kernels: 46.8 us -> 44.1 us  [the longest x1 43.5 us: shards(): pl.pallas_call(functools.partial(kernel, sizes), out_shape=(pltpu.VMEM((2...]
    unnamed x2 -> x0, local copies, waits for them, and re-layouts: 2.62 us -> none
where the time goes in v1:
time: 44.9 us; the launch traced here: 44.7 us
  Pallas kernels  44.1 us (98%)
  between operations  0.64 us (1%)
    pallas_call x1, Pallas kernels, shards(): pl.pallas_call(functools.partial(kernel, sizes), out_shape=(pltpu.VMEM((2...  43.5 us

profile of v1, /device:TPU:1, one launch (start us, length us, event | category | flops | bytes accessed | tf_op | source)
XLA Modules:
  0.0 44.7 jit_solution(6497617397028641908)
XLA Ops:
  0.6 43.5 %shard_map.104 = (f32[24,128]{1,0:T(8,128)S(1)}, f32[24,128]{1,0:T(8,128)S(1)}) custom-call(f32[24,128]{1,0:T(8,128)} %bitcast.15, f32[144,128]{1,0:T(8,128)} %bitcast.14, bf16[576,128]{1,0:T(8,128)(2,1)} %bitcast.12, f32[2592,128]{1,0:T(8,128)} %bitcast.10, f32[288,128]{1,0:T(8,128)} %bitcast.13, f32[756,1,128]{2,1,0:T(1,128)} %bitcast.11, ...), custom_call_target="tpu_custom_call" | custom-call | tf_op jit(solution)/shard_map/pallas_call | solution.py:559
  44.1 0.6 %shard_map.105 = (f32[24,128]{1,0:T(8,128)}, f32[24,128]{1,0:T(8,128)}) custom-call(f32[24,128]{1,0:T(8,128)S(1)} %get-tuple-element.6.sol_v, f32[24,128]{1,0:T(8,128)S(1)} %get-tuple-element.7.res_v), custom_call_target="tpu_custom_call" | custom-call | tf_op jit(solution)/shard_map/pallas_call | solution.py:592

commit v2 on v1

v2 whole, which is shorter than its diff:
```python
import functools

import jax
import jax.numpy as jnp
from jax import lax
from jax.experimental import pallas as pl
from jax.experimental.pallas import tpu as pltpu
from jax.sharding import PartitionSpec as P

MESH = pl.DeviceIdType.MESH
F32 = jnp.float32
BF16 = jnp.bfloat16

DIAGONAL = 4.1
TWIST = 0.1
DENOMINATOR = DIAGONAL * DIAGONAL + TWIST * TWIST
PRE_SAME = 0.8 * DIAGONAL / DENOMINATOR
PRE_OTHER = 0.8 * TWIST / DENOMINATOR

STEPS = ((1, 0, 0), (-1, 0, 0), (0, 1, 0), (0, -1, 0), (0, 0, 1), (0, 0, -1))
NEAR = ((0, 0, 0),) + STEPS


def added(one, other):
    return tuple(a + b for a, b in zip(one, other))


def plan(sizes):
    def wrapped(offset):
        return tuple(o % n for o, n in zip(offset, sizes))

    slots = {}
    for one in NEAR:
        for other in NEAR:
            slots.setdefault(wrapped(added(one, other)), len(slots))
    plane = {}
    for dt in range(sizes[0]):
        for dz in range(sizes[1]):
            plane[(dt, dz, 0)] = len(plane)
    line = {(0, 0, dx): dx for dx in range(sizes[2])}
    return wrapped, slots, plane, line


def pieces(value):
    high = value.astype(BF16)
    rest = value - high.astype(F32)
    middle = rest.astype(BF16)
    low = (rest - middle.astype(F32)).astype(BF16)
    return high, middle, low


def row_sums(value):
    ones = jnp.ones((8, 384), BF16)
    dims = (((1,), (1,)), ((), ()))
    stacked = jnp.concatenate(pieces(value), axis=1)
    return lax.dot_general(ones, stacked, dims, preferred_element_type=F32)


def lanes_from(value, places):
    return jnp.take_along_axis(
        value, jnp.broadcast_to(places, value.shape), axis=1, mode="promise_in_bounds"
    )


def four_groups(value):
    return (value + pltpu.roll(value, 32, 1)) + (pltpu.roll(value, 64, 1) + pltpu.roll(value, 96, 1))


def four_lanes(value, first):
    one, two, three, four = (lanes_from(value, first + b) for b in range(4))
    return (one + two) + (three + four)


def distance(offset, sizes):
    t, z, x = (min(o % n, n - o % n) for o, n in zip(offset, sizes))
    return t / 2 + (t % 2) / 2 + z + x


def kernel(
    sizes,
    src_h, gauge_h, fine_h, mblk_h, mvec_h, bblk_h,
    sol_ref, res_ref,
    src, gauge, fine, mblk, mvec, bblk,
    halo, half_out, hop_rows, first, second, fine_f, mv_parts, own_blk, got_blk, near_blk,
    right_rows, sum_rows, around, plane_rows, line_rows, mid, wide, final,
    local_sem, halo_send, halo_recv, blk_send, blk_recv, right_send, right_recv,
    plane_send, plane_recv, line_send, line_recv, mid_send, mid_recv, mid_line_send, mid_line_recv,
    near_token, far_token,
):
    wrapped, slots, plane, line = plan(sizes)
    here = tuple(lax.axis_index(axis) for axis in ("ta", "gz", "xy"))

    def at(offset):
        return tuple(
            h if o % n == 0 else lax.rem(h + (o % n), n) for h, o, n in zip(here, offset, sizes)
        )

    def against(offset):
        return at(tuple(-o for o in offset))

    loads = [
        pltpu.make_async_copy(a, b, local_sem.at[i])
        for i, (a, b) in enumerate(
            (
                (src_h, src), (gauge_h, gauge), (bblk_h, bblk), (fine_h, fine), (mvec_h, mvec),
                (mblk_h, mblk),
            )
        )
    ]
    for load in loads:
        load.start()

    barrier = pltpu.get_barrier_semaphore()
    for step in STEPS:
        pl.semaphore_signal(barrier, inc=1, device_id=at(step), device_id_type=MESH)

    def remote(source, target, send, recv, device):
        return pltpu.make_async_remote_copy(
            src_ref=source, dst_ref=target, send_sem=send, recv_sem=recv,
            device_id=device, device_id_type=MESH,
        )

    class Group:
        def __init__(self, source, target, send, recv, places):
            places = sorted(places, key=lambda place: -distance(place[0], sizes))
            self.all = [
                remote(
                    source(slot) if callable(source) else source, target.at[pl.ds(slot, 1)],
                    send, recv, against(offset),
                )
                for offset, slot in places
            ]
            low = min(slot for _, slot in places)
            whole = target.at[pl.ds(low, len(places))]
            self.sum = remote(whole, whole, send, recv, here)

        def start(self):
            for copy in self.all:
                copy.start()
            return self

        def arrived(self):
            self.sum.wait_recv()

        def sent(self):
            self.sum.wait_send()

    def greet(offsets, token):
        far = [offset for offset in offsets if any(wrapped(offset))]
        for offset in far:
            pl.semaphore_signal(token, inc=1, device_id=at(offset), device_id_type=MESH)
        return len(far)

    six = [(STEPS[d], d) for d in range(6)]

    rows12 = lax.broadcasted_iota(jnp.int32, (12, 128), 0)
    chiral = jnp.where(rows12 < 6, 1.0, -1.0).astype(F32)

    def smoothed(re, im):
        return (
            PRE_SAME * re + PRE_OTHER * (chiral * im),
            PRE_SAME * im - PRE_OTHER * (chiral * re),
        )

    def send_halves(which, field):
        r0, r1, r2, r3 = (field[pl.ds(s * 3, 3), :] for s in range(4))
        i0, i1, i2, i3 = (field[pl.ds(12 + s * 3, 3), :] for s in range(4))
        for axis, lower in enumerate(
            (
                (r2, r3, i2, i3),
                (-i2, i3, r2, -r3),
                (-i3, -i2, r3, r2),
                (-r3, r2, -i3, i2),
            )
        ):
            for d in (2 * axis, 2 * axis + 1):
                for row, (up, low) in enumerate(zip((r0, r1, i0, i1), lower)):
                    value = up - low if d % 2 == 0 else up + low
                    if axis < 3:
                        half_out[which, d, pl.ds(row * 3, 3), :] = value
                    else:
                        shift = 127 if d == 6 else 1
                        halo[which, d, pl.ds(row * 3, 3), :] = pltpu.roll(value, shift, 1)

    loads[0].wait()
    first_re, first_im = smoothed(src[0:12, :], src[12:24, :])
    first[0:12, :] = first_re
    first[12:24, :] = first_im
    send_halves(0, first)
    pl.semaphore_wait(barrier, len(STEPS))
    first_copies = Group(
        lambda d: half_out.at[0, pl.ds(d, 1)], halo.at[0], halo_send.at[0], halo_recv.at[0], six
    ).start()

    lanes8 = lax.broadcasted_iota(jnp.int32, (8, 128), 1)
    lane_row = lax.broadcasted_iota(jnp.int32, (1, 128), 1)
    near_blk[...] = jnp.zeros_like(near_blk)
    own_blk[...] = jnp.zeros_like(own_blk)
    around[...] = jnp.zeros_like(around)
    sum_rows[...] = jnp.zeros_like(sum_rows)
    right_rows[pl.ds(0, 1), :] = jnp.zeros((1, 128), F32)
    mv_parts[...] = jnp.zeros_like(mv_parts)
    loads[2].wait()
    per_x = bblk.shape[0] // 14

    def site_blocks(x):
        start = (x * 9) // 2
        skipped = lax.rem(x, 2) * 64
        rows = [
            [bblk[pl.ds(p * 7 * per_x + start + q, 7, stride=per_x), 0, :] for q in range(5)]
            for p in range(2)
        ]
        lane = lax.broadcasted_iota(jnp.int32, (7, 128), 1)
        for c in range(6):
            place = lax.rem(lane, 32) * 24 + 4 * c + lane // 32 + skipped
            chunk = place // 128
            within = lax.rem(place, 128)
            valid = lax.rem(lane, 32) < 24
            for p in range(2):
                value = jnp.zeros((7, 128), F32)
                for q in range(5):
                    value = jnp.where(chunk == q, lanes_from(rows[p][q], within), value)
                yield p, c, jnp.where(valid, value, 0.0)

    for p, q, value in site_blocks(here[2]):
        own_blk[0, p, q, pl.ds(0, 7), :] = value
        near_blk[p, q, pl.ds(0, 7, stride=8), :] = value
    for d in (4, 5):
        for p, q, value in site_blocks(at(STEPS[d])[2]):
            near_blk[p, q, pl.ds(1 + d, 7, stride=8), :] = value
    loads[3].wait()
    fine_f[...] = fine[...].astype(F32)
    loads[4].wait()
    for p in range(2):
        for c in range(6):
            block = mvec[pl.ds(p * 144 + c, 24, stride=6), :]
            high = block.astype(BF16)
            mv_parts[p, 0, pl.ds(0, 24), pl.ds(c * 128, 128)] = high
            mv_parts[p, 1, pl.ds(0, 24), pl.ds(c * 128, 128)] = (block - high.astype(F32)).astype(BF16)

    direction = lax.broadcasted_iota(jnp.int32, (8, 128), 0)
    is_t = direction < 2
    is_z = direction < 4
    is_x = direction < 6
    odd_one = lax.rem(direction, 2) == 1
    base = jnp.where(odd_one, 1.0, -1.0).astype(F32)
    in_z = jnp.logical_and(is_z, jnp.logical_not(is_t))
    in_x = jnp.logical_and(is_x, jnp.logical_not(is_z))
    in_y = jnp.logical_not(is_x)

    def flipped(mask):
        return jnp.where(mask, -base, base)

    sign_e = flipped(jnp.logical_or(in_z, in_x))
    sign_f = flipped(jnp.logical_or(in_z, in_y))
    sign_g = flipped(jnp.logical_or(in_x, in_y))

    def pick(a, b, c, d):
        return jnp.where(is_t, a, jnp.where(is_z, b, jnp.where(is_x, c, d)))

    loads[1].wait()

    def hopping(which):
        link = [
            [[gauge[pl.ds(p * 72 + c * 3 + e, 8, stride=9), :] for e in range(3)] for c in range(3)]
            for p in range(2)
        ]
        half = [
            [[halo[which, :, p * 6 + s * 3 + c, :] for c in range(3)] for s in range(2)]
            for p in range(2)
        ]

        def put(p, s, c, value):
            hop_rows[pl.ds(p * 12 + s * 3 + c, 1), :] = jnp.sum(value, axis=0, keepdims=True)

        for c in range(3):
            moved = [[0.0, 0.0], [0.0, 0.0]]
            for s in range(2):
                for e in range(3):
                    lr, li = link[0][c][e], link[1][c][e]
                    hr, hi = half[0][s][e], half[1][s][e]
                    moved[0][s] = moved[0][s] + (lr * hr - li * hi)
                    moved[1][s] = moved[1][s] + (lr * hi + li * hr)
            (a0, a1), (b0, b1) = moved
            put(0, 0, c, a0)
            put(0, 1, c, a1)
            put(1, 0, c, b0)
            put(1, 1, c, b1)
            put(0, 2, c, base * pick(a0, b0, b1, a1))
            put(1, 2, c, sign_e * pick(b0, a0, a1, b1))
            put(0, 3, c, sign_f * pick(a1, b1, b0, a0))
            put(1, 3, c, sign_g * pick(b1, a1, a0, b0))

    def residual(re, im):
        hop_re, hop_im = hop_rows[0:12, :], hop_rows[12:24, :]
        out_re = src[0:12, :] - (DIAGONAL * re - TWIST * (chiral * im) - 0.5 * hop_re)
        out_im = src[12:24, :] - (DIAGONAL * im + TWIST * (chiral * re) - 0.5 * hop_im)
        return out_re, out_im

    first_copies.arrived()
    near_count = greet([(2, 0, 0), (-2, 0, 0), (0, 0, 2), (0, 0, -2)], near_token)
    hopping(0)
    left_re, left_im = smoothed(*residual(first_re, first_im))
    second_re, second_im = first_re + left_re, first_im + left_im
    second[0:12, :] = second_re
    second[12:24, :] = second_im
    send_halves(1, second)
    second_copies = Group(
        lambda d: half_out.at[1, pl.ds(d, 1)], halo.at[1], halo_send.at[1], halo_recv.at[1], six
    ).start()
    blk_copies = Group(own_blk, got_blk, blk_send, blk_recv, six[:4]).start()

    second_copies.arrived()
    hopping(1)
    res_re, res_im = residual(second_re, second_im)
    res_ref[0:12, :] = res_re
    res_ref[12:24, :] = res_im
    hop_rows[0:12, :] = res_re.astype(BF16).astype(F32)
    hop_rows[12:24, :] = res_im.astype(BF16).astype(F32)

    def fine_vector(p, s, c):
        return fine_f[pl.ds(p * 288 + c * 4 + s, 24, stride=12), :]

    part_re = jnp.zeros((24, 128), F32)
    part_im = jnp.zeros((24, 128), F32)
    for s in range(4):
        for c in range(3):
            vr, vi = fine_vector(0, s, c), fine_vector(1, s, c)
            rr = hop_rows[pl.ds(s * 3 + c, 1), :]
            ri = hop_rows[pl.ds(12 + s * 3 + c, 1), :]
            part_re = part_re + (vr * rr + vi * ri)
            part_im = part_im + (vr * ri - vi * rr)
    parts = jnp.concatenate([part_re, part_im], axis=0)
    wide[0:48, :] = four_lanes(parts, 4 * lax.rem(lane_row, 32))

    def middle_row(p, c):
        rows = [wide[pl.ds(p * 24 + c * 4 + g, 1), :] for g in range(4)]
        return jnp.where(
            lane_row < 64,
            jnp.where(lane_row < 32, rows[0], rows[1]),
            jnp.where(lane_row < 96, rows[2], rows[3]),
        )

    q_re = jnp.zeros((24, 128), F32)
    q_im = jnp.zeros((24, 128), F32)
    for c in range(6):
        vr = mvec[pl.ds(c, 24, stride=6), :]
        vi = mvec[pl.ds(144 + c, 24, stride=6), :]
        mr, mi = middle_row(0, c), middle_row(1, c)
        q_re = q_re + (vr * mr + vi * mi)
        q_im = q_im + (vr * mi - vi * mr)
    sum_rows[0:24, :] = q_re
    sum_rows[32:56, :] = q_im
    right_rows[pl.ds(0, 1), pl.ds(0, 64)] = row_sums(sum_rows[...])[0:1]

    if near_count:
        pl.semaphore_wait(near_token, near_count)
    right_copies = Group(
        right_rows.at[pl.ds(0, 1)], right_rows, right_send, right_recv, [o for o in slots.items() if o[1]]
    ).start()
    final[pl.ds(96, 48), :] = 0.4 * four_lanes(parts, 4 * (lane_row // 4))
    blk_copies.arrived()
    for d in range(4):
        for p in range(2):
            for q in range(6):
                near_blk[p, q, pl.ds(1 + d, 7, stride=8), :] = got_blk[d, p, q, pl.ds(0, 7), :]
    right_copies.arrived()
    far_count = greet([(4, 0, 0), (-4, 0, 0)], far_token)

    for d in range(7):
        for i in range(7):
            slot = slots[wrapped(added(NEAR[d], NEAR[i]))]
            around[pl.ds(d * 8 + i, 1), :] = right_rows[pl.ds(slot, 1), :]
    rows_now = around[...]
    sum_re = jnp.zeros((8, 128), F32)
    sum_im = jnp.zeros((8, 128), F32)
    for c in range(6):
        xr = lanes_from(rows_now, 4 * c + lane_row // 32)
        xi = lanes_from(rows_now, 32 + 4 * c + lane_row // 32)
        br, bi = near_blk[0, c], near_blk[1, c]
        term_re = br * xr - bi * xi
        term_im = br * xi + bi * xr
        for d in range(7):
            sum_re = sum_re + term_re[d * 8:(d + 1) * 8]
            sum_im = sum_im + term_im[d * 8:(d + 1) * 8]
    right_re = lanes_from(rows_now[0:8], lax.rem(lane_row, 32))
    right_im = lanes_from(rows_now[0:8], 32 + lax.rem(lane_row, 32))
    one_re = 2.0 * right_re + four_groups(sum_re)
    one_im = 2.0 * right_im + four_groups(sum_im)

    sum_re = jnp.zeros((8, 128), F32)
    sum_im = jnp.zeros((8, 128), F32)
    for c in range(6):
        xr = lanes_from(one_re, 4 * c + lane_row // 32)
        xi = lanes_from(one_im, 4 * c + lane_row // 32)
        br, bi = own_blk[0, 0, c], own_blk[0, 1, c]
        sum_re = sum_re + (br * xr - bi * xi)
        sum_im = sum_im + (br * xi + bi * xr)
    two = four_groups(
        jnp.concatenate(
            [jnp.sum(sum_re, axis=0, keepdims=True), jnp.sum(sum_im, axis=0, keepdims=True)], axis=0
        )
    )
    fr, fi = one_re[0:1], one_im[0:1]
    sr = 2.0 * fr + two[0:1]
    si = 2.0 * fi + two[1:2]
    rr, ri = right_re[0:1], right_im[0:1]
    products = (
        fr * fr + fi * fi,
        sr * sr + si * si,
        fr * sr + fi * si,
        fr * si - fi * sr,
        fr * rr + fi * ri,
        fr * ri - fi * rr,
        sr * rr + si * ri,
        sr * ri - si * rr,
    )
    folded = jnp.concatenate(products, axis=0)
    folded = folded + pltpu.roll(folded, 16, 1)
    rows8 = lax.broadcasted_iota(jnp.int32, (8, 128), 0)
    folded = jnp.where(lanes8 // 16 == rows8, folded, 0.0)
    line_rows[pl.ds(0, 1), :] = jnp.sum(folded, axis=0, keepdims=True)
    line_copies = Group(
        line_rows.at[pl.ds(0, 1)], line_rows, line_send, line_recv, [o for o in line.items() if o[1]]
    ).start()

    left = jnp.concatenate([rr, ri, fr, fi], axis=0)
    turned = jnp.concatenate([-ri, rr, -fi, fr], axis=0)
    guess = jnp.zeros((4, 768), F32)
    for p, rows in ((0, left), (1, turned)):
        high = rows.astype(BF16)
        low = (rows - high.astype(F32)).astype(BF16)
        guess = guess + jnp.dot(high[:, 0:32], mv_parts[p, 0], preferred_element_type=F32)
        guess = guess + jnp.dot(low[:, 0:32], mv_parts[p, 0], preferred_element_type=F32)
        guess = guess + jnp.dot(high[:, 0:32], mv_parts[p, 1], preferred_element_type=F32)
    mid[0] = guess
    mid_copies = Group(
        mid.at[pl.ds(0, 1)], mid, mid_send, mid_recv, [(STEPS[d], 1 + d) for d in range(4)]
    ).start()
    lanes4 = lax.broadcasted_iota(jnp.int32, (4, 128), 1)
    place4 = lax.rem(lanes4, 32)
    for c in range(6):
        now = guess[:, c * 128:(c + 1) * 128]
        mid[7, :, pl.ds(c * 128, 128)] = jnp.where(
            place4 == 31, pltpu.roll(now, 31, 1), pltpu.roll(now, 127, 1)
        )
        mid[8, :, pl.ds(c * 128, 128)] = jnp.where(
            place4 == 0, pltpu.roll(now, 97, 1), pltpu.roll(now, 1, 1)
        )
    loads[5].wait()

    def middle_step(d, sums):
        sums = list(sums)
        for c in range(6):
            br = mblk[pl.ds(d * 144 + c, 24, stride=6), :]
            bi = mblk[pl.ds((9 + d) * 144 + c, 24, stride=6), :]
            for v in range(2):
                xr = mid[d, pl.ds(2 * v, 1), pl.ds(c * 128, 128)]
                xi = mid[d, pl.ds(2 * v + 1, 1), pl.ds(c * 128, 128)]
                sums[2 * v] = sums[2 * v] + (br * xr - bi * xi)
                sums[2 * v + 1] = sums[2 * v + 1] + (br * xi + bi * xr)
        return tuple(sums)

    sums = tuple(jnp.zeros((24, 128), F32) for _ in range(4))
    sums = middle_step(0, sums)
    sums = lax.fori_loop(7, 9, middle_step, sums)

    line_copies.arrived()
    plane_rows[pl.ds(0, 1), :] = jnp.sum(line_rows[...], axis=0, keepdims=True)
    if far_count:
        pl.semaphore_wait(far_token, far_count)
    plane_copies = Group(
        plane_rows.at[pl.ds(0, 1)], plane_rows, plane_send, plane_recv, [o for o in plane.items() if o[1]]
    ).start()

    mid_line_copies = Group(
        mid.at[pl.ds(0, 1)], mid, mid_line_send, mid_line_recv,
        [(STEPS[d], 1 + d) for d in (4, 5)],
    ).start()
    mid_copies.arrived()
    sums = lax.fori_loop(1, 5, middle_step, sums)
    mid_line_copies.arrived()
    sums = lax.fori_loop(5, 7, middle_step, sums)
    rows24 = lax.broadcasted_iota(jnp.int32, (24, 128), 0)
    lanes24 = lax.broadcasted_iota(jnp.int32, (24, 128), 1)
    mine = lax.rem(rows24, 4) == lanes24 // 32
    for i in range(4):
        for c in range(6):
            wide[pl.ds(i * 24 + c * 4, 4), :] = jnp.broadcast_to(
                mid[0, pl.ds(i, 1), pl.ds(c * 128, 128)], (4, 128)
            )
    changes = [
        0.2 * jnp.where(mine, wide[pl.ds(i * 24, 24), :], 0.0) - 0.4 * sums[i] for i in range(4)
    ]
    final[pl.ds(0, 96), :] = lanes_from(
        four_groups(jnp.concatenate(changes, axis=0)), lane_row // 4
    )

    plane_copies.arrived()
    totals = jnp.broadcast_to(jnp.sum(plane_rows[...], axis=0, keepdims=True), (8, 128))
    totals = jnp.sum(jnp.where(lanes8 // 16 == rows8, totals, 0.0), axis=1, keepdims=True)
    first_norm, second_norm, cross_re, cross_im, ar, ai, br, bi = (
        jnp.broadcast_to(totals[i:i + 1, :], (1, 128)) for i in range(8)
    )
    determinant = first_norm * second_norm - cross_re * cross_re - cross_im * cross_im
    one_r = (second_norm * ar - (cross_re * br - cross_im * bi)) / determinant
    one_i = (second_norm * ai - (cross_re * bi + cross_im * br)) / determinant
    two_r = (first_norm * br - (cross_re * ar + cross_im * ai)) / determinant
    two_i = (first_norm * bi - (cross_re * ai - cross_im * ar)) / determinant
    ur, ui, wr, wi = (final[pl.ds(i * 24, 24), :] for i in range(4))
    update_re = final[96:120, :] + (one_r * ur - one_i * ui) + (two_r * wr - two_i * wi)
    update_im = final[120:144, :] + (one_r * ui + one_i * ur) + (two_r * wi + two_i * wr)
    update_re = update_re.astype(BF16).astype(F32)
    update_im = update_im.astype(BF16).astype(F32)
    for s in range(4):
        for c in range(3):
            vr, vi = fine_vector(0, s, c), fine_vector(1, s, c)
            add_re = jnp.sum(vr * update_re - vi * update_im, axis=0, keepdims=True)
            add_im = jnp.sum(vr * update_im + vi * update_re, axis=0, keepdims=True)
            row = s * 3 + c
            sol_ref[pl.ds(row, 1), :] = second[pl.ds(row, 1), :] + add_re
            sol_ref[pl.ds(12 + row, 1), :] = second[pl.ds(12 + row, 1), :] + add_im

    for group in (
        first_copies, second_copies, blk_copies, right_copies, line_copies, mid_copies, plane_copies,
        mid_line_copies,
    ):
        group.sent()


def deliver(sol_v, res_v, sol_h, res_h, sem):
    copies = (
        pltpu.make_async_copy(sol_v, sol_h, sem.at[0]),
        pltpu.make_async_copy(res_v, res_h, sem.at[1]),
    )
    for copy in copies:
        copy.start()
    for copy in copies:
        copy.wait()


def solution(mesh):
    sizes = tuple(mesh.shape[axis] for axis in ("ta", "gz", "xy"))
    slots = plan(sizes)[1]

    def shards(source_field, gauge_links, fine_vectors, middle_blocks, middle_vectors, bottom_blocks):
        fine = jnp.transpose(fine_vectors, (0, 1, 3, 4, 5, 6, 2, 7)).reshape(576, 128)
        operands = (
            source_field.reshape(24, 128),
            gauge_links.reshape(144, 128),
            fine,
            middle_blocks.reshape(2592, 128),
            middle_vectors.reshape(288, 128),
            bottom_blocks.reshape(-1, 1, 128),
        )
        vmem = [pltpu.VMEM(o.shape, o.dtype) for o in operands]
        dma = pltpu.SemaphoreType.DMA
        sol, res = pl.pallas_call(
            functools.partial(kernel, sizes),
            out_shape=(pltpu.VMEM((24, 128), F32),) * 2,
            in_specs=[pl.BlockSpec(memory_space=pltpu.HBM)] * len(operands),
            out_specs=(pl.BlockSpec(memory_space=pltpu.VMEM),) * 2,
            scratch_shapes=vmem
            + [
                pltpu.VMEM((2, 8, 12, 128), F32),
                pltpu.VMEM((2, 6, 12, 128), F32),
                pltpu.VMEM((24, 128), F32),
                pltpu.VMEM((24, 128), F32),
                pltpu.VMEM((24, 128), F32),
                pltpu.VMEM((576, 128), F32),
                pltpu.VMEM((2, 2, 32, 768), BF16),
                pltpu.VMEM((1, 2, 6, 8, 128), F32),
                pltpu.VMEM((4, 2, 6, 8, 128), F32),
                pltpu.VMEM((2, 6, 56, 128), F32),
                pltpu.VMEM((len(slots), 128), F32),
                pltpu.VMEM((64, 128), F32),
                pltpu.VMEM((56, 128), F32),
                pltpu.VMEM((sizes[0] * sizes[1], 128), F32),
                pltpu.VMEM((sizes[2], 128), F32),
                pltpu.VMEM((9, 4, 768), F32),
                pltpu.VMEM((96, 128), F32),
                pltpu.VMEM((144, 128), F32),
                dma((len(operands),)),
                dma((2,)),
                dma((2,)),
            ]
            + [dma] * 12
            + [pltpu.SemaphoreType.REGULAR] * 2,
            compiler_params=pltpu.CompilerParams(collective_id=0, has_side_effects=True),
        )(*operands)
        sol, res = pl.pallas_call(
            deliver,
            out_shape=(jax.ShapeDtypeStruct((24, 128), F32),) * 2,
            in_specs=[pl.BlockSpec(memory_space=pltpu.VMEM)] * 2,
            out_specs=(pl.BlockSpec(memory_space=pltpu.HBM),) * 2,
            scratch_shapes=[pltpu.SemaphoreType.DMA((2,))],
        )(*(pltpu.with_memory_space_constraint(o, pltpu.VMEM) for o in (sol, res)))
        return sol.reshape(source_field.shape), res.reshape(source_field.shape)

    return jax.shard_map(
        shards,
        mesh=mesh,
        in_specs=(
            P(None, None, None, "ta", "gz", "xy", None),
            P(None, None, None, None, "ta", "gz", "xy", None),
            P(None, None, None, None, "ta", "gz", "xy", None),
            P(None, None, None, "ta", "gz", "xy", None),
            P(None, None, "ta", "gz", "xy", None),
            P(None, None, "ta", "gz", None),
        ),
        out_specs=(
            P(None, None, None, "ta", "gz", "xy", None),
            P(None, None, None, "ta", "gz", "xy", None),
        ),
        check_vma=False,
    )
```

time: 44.9 us -> 43.8 us (0.976)
  Pallas kernels: 44.1 us -> 43 us
    pallas_call x1, Pallas kernels: 43.5 us -> 42.4 us  [shards(): pl.pallas_call(functools.partial(kernel, sizes), out_shape=(pltpu.VMEM((2...]
where the time goes in v2:
time: 43.8 us; the launch traced here: 43.6 us
  Pallas kernels  43 us (98%)
  between operations  0.64 us (1%)
    pallas_call x1, Pallas kernels, shards(): pl.pallas_call(functools.partial(kernel, sizes), out_shape=(pltpu.VMEM((2...  42.4 us

profile of v2, /device:TPU:1, one launch (start us, length us, event | category | flops | bytes accessed | tf_op | source)
XLA Modules:
  0.0 43.6 jit_solution(17903655354185342188)
XLA Ops:
  0.6 42.4 %shard_map.77 = (f32[24,128]{1,0:T(8,128)S(1)}, f32[24,128]{1,0:T(8,128)S(1)}) custom-call(f32[24,128]{1,0:T(8,128)} %bitcast.15, f32[144,128]{1,0:T(8,128)} %bitcast.14, bf16[576,128]{1,0:T(8,128)(2,1)} %bitcast.12, f32[2592,128]{1,0:T(8,128)} %bitcast.10, f32[288,128]{1,0:T(8,128)} %bitcast.13, f32[756,1,128]{2,1,0:T(1,128)} %bitcast.11), custom_call_target="tpu_custom_call" | custom-call | tf_op jit(solution)/shard_map/pallas_call | solution.py:558
  43.0 0.6 %shard_map.78 = (f32[24,128]{1,0:T(8,128)}, f32[24,128]{1,0:T(8,128)}) custom-call(f32[24,128]{1,0:T(8,128)S(1)} %get-tuple-element.6.sol_v, f32[24,128]{1,0:T(8,128)S(1)} %get-tuple-element.7.res_v), custom_call_target="tpu_custom_call" | custom-call | tf_op jit(solution)/shard_map/pallas_call | solution.py:591

commit v3 on v2

--- a/solution.py
+++ b/solution.py
@@ -19,6 +19,7 @@
 
 STEPS = ((1, 0, 0), (-1, 0, 0), (0, 1, 0), (0, -1, 0), (0, 0, 1), (0, 0, -1))
 NEAR = ((0, 0, 0),) + STEPS
+TARGETS = ((0, 1, 0), (2, 0, 0), (2, 1, 0))
 
 
 def added(one, other):
@@ -85,7 +86,7 @@
     right_rows, sum_rows, around, plane_rows, line_rows, mid, wide, final,
     local_sem, halo_send, halo_recv, blk_send, blk_recv, right_send, right_recv,
     plane_send, plane_recv, line_send, line_recv, mid_send, mid_recv, mid_line_send, mid_line_recv,
-    near_token, far_token,
+    near_token, far_token, all_rows, total_row, all_send, all_recv,
 ):
     wrapped, slots, plane, line = plan(sizes)
     here = tuple(lax.axis_index(axis) for axis in ("ta", "gz", "xy"))
@@ -114,6 +115,36 @@
     for step in STEPS:
         pl.semaphore_signal(barrier, inc=1, device_id=at(step), device_id_type=MESH)
 
+    def is_here(place):
+        same = [h == o for h, o in zip(here, place)]
+        return jnp.logical_and(jnp.logical_and(same[0], same[1]), same[2])
+
+    targets = [t for t in TARGETS if all(o < n for o, n in zip(t, sizes))]
+    chosen = [is_here(t) for t in targets]
+    served = functools.reduce(jnp.logical_or, chosen)
+    squares = sizes[0] * sizes[1]
+    for target, mine in zip(targets, chosen):
+
+        @pl.when(mine)
+        def _(target=target):
+            def greet_square(i, _):
+                square = lax.rem(i + squares // 2, squares)
+                place = lax.rem(target[0] + square // sizes[1], sizes[0])
+                other = lax.rem(target[1] + lax.rem(square, sizes[1]), sizes[1])
+                for dx in range(sizes[2]):
+
+                    def signal(dx=dx):
+                        device = (place, other, (target[2] + dx) % sizes[2])
+                        pl.semaphore_signal(barrier, inc=1, device_id=device, device_id_type=MESH)
+
+                    if dx:
+                        signal()
+                    else:
+                        pl.when(square != 0)(signal)
+                return 0
+
+            lax.fori_loop(0, squares, greet_square, 0)
+
     def remote(source, target, send, recv, device):
         return pltpu.make_async_remote_copy(
             src_ref=source, dst_ref=target, send_sem=send, recv_sem=recv,
@@ -121,7 +152,8 @@
         )
 
     class Group:
-        def __init__(self, source, target, send, recv, places):
+        def __init__(self, source, target, send, recv, places, spared=()):
+            self.spared = spared
             places = sorted(places, key=lambda place: -distance(place[0], sizes))
             self.all = [
                 remote(
@@ -130,13 +162,18 @@
                 )
                 for offset, slot in places
             ]
+            self.reached = [against(offset) for offset, _ in places]
             low = min(slot for _, slot in places)
             whole = target.at[pl.ds(low, len(places))]
             self.sum = remote(whole, whole, send, recv, here)
 
         def start(self):
-            for copy in self.all:
-                copy.start()
+            for copy, (t, z, _) in zip(self.all, self.reached):
+                if self.spared:
+                    clear = [t * sizes[1] + z != square for square in self.spared]
+                    pl.when(functools.reduce(jnp.logical_and, clear))(copy.start)
+                else:
+                    copy.start()
             return self
 
         def arrived(self):
@@ -187,7 +224,7 @@
     first[0:12, :] = first_re
     first[12:24, :] = first_im
     send_halves(0, first)
-    pl.semaphore_wait(barrier, len(STEPS))
+    pl.semaphore_wait(barrier, len(STEPS) + len(targets) - served.astype(jnp.int32))
     first_copies = Group(
         lambda d: half_out.at[0, pl.ds(d, 1)], halo.at[0], halo_send.at[0], halo_recv.at[0], six
     ).start()
@@ -420,6 +457,19 @@
     rows8 = lax.broadcasted_iota(jnp.int32, (8, 128), 0)
     folded = jnp.where(lanes8 // 16 == rows8, folded, 0.0)
     line_rows[pl.ds(0, 1), :] = jnp.sum(folded, axis=0, keepdims=True)
+    def copy_to(target):
+        t, z, x = (lax.rem(h + n - o, n) for h, o, n in zip(here, target, sizes))
+        row = (t * sizes[1] + z) * sizes[2] + x
+        return remote(
+            line_rows.at[pl.ds(0, 1)], all_rows.at[pl.ds(row, 1), 0], all_send.at[0], all_recv.at[0], target
+        )
+
+    for target, mine in zip(targets, chosen):
+
+        @pl.when(jnp.logical_not(mine))
+        def _(target=target):
+            copy_to(target).start()
+
     line_copies = Group(
         line_rows.at[pl.ds(0, 1)], line_rows, line_send, line_recv, [o for o in line.items() if o[1]]
     ).start()
@@ -469,8 +519,16 @@
     plane_rows[pl.ds(0, 1), :] = jnp.sum(line_rows[...], axis=0, keepdims=True)
     if far_count:
         pl.semaphore_wait(far_token, far_count)
+    spared = [
+        jnp.where(
+            jnp.logical_and(here[2] == target[2], jnp.logical_not(mine)),
+            target[0] * sizes[1] + target[1], -1,
+        )
+        for target, mine in zip(targets, chosen)
+    ]
     plane_copies = Group(
-        plane_rows.at[pl.ds(0, 1)], plane_rows, plane_send, plane_recv, [o for o in plane.items() if o[1]]
+        plane_rows.at[pl.ds(0, 1)], plane_rows, plane_send, plane_recv, [o for o in plane.items() if o[1]],
+        spared,
     ).start()
 
     mid_line_copies = Group(
@@ -496,8 +554,21 @@
         four_groups(jnp.concatenate(changes, axis=0)), lane_row // 4
     )
 
-    plane_copies.arrived()
-    totals = jnp.broadcast_to(jnp.sum(plane_rows[...], axis=0, keepdims=True), (8, 128))
+    everyone = squares * sizes[2]
+
+    @pl.when(served)
+    def _():
+        whole = all_rows.at[pl.ds(1, everyone - 1)]
+        remote(whole, whole, all_send.at[0], all_recv.at[0], here).wait_recv()
+        all_rows[pl.ds(0, 1)] = line_rows[pl.ds(0, 1), :].reshape(1, 1, 128)
+        total_row[...] = jnp.sum(all_rows[...].reshape(everyone, 128), axis=0, keepdims=True)
+
+    @pl.when(jnp.logical_not(served))
+    def _():
+        plane_copies.arrived()
+        total_row[...] = jnp.sum(plane_rows[...], axis=0, keepdims=True)
+
+    totals = jnp.broadcast_to(total_row[...], (8, 128))
     totals = jnp.sum(jnp.where(lanes8 // 16 == rows8, totals, 0.0), axis=1, keepdims=True)
     first_norm, second_norm, cross_re, cross_im, ar, ai, br, bi = (
         jnp.broadcast_to(totals[i:i + 1, :], (1, 128)) for i in range(8)
@@ -522,10 +593,23 @@
             sol_ref[pl.ds(12 + row, 1), :] = second[pl.ds(12 + row, 1), :] + add_im
 
     for group in (
-        first_copies, second_copies, blk_copies, right_copies, line_copies, mid_copies, plane_copies,
+        first_copies, second_copies, blk_copies, right_copies, line_copies, mid_copies,
         mid_line_copies,
     ):
         group.sent()
+    left_out = sum((square >= 0).astype(jnp.int32) for square in spared)
+    for n in range(len(targets) + 1):
+
+        @pl.when(left_out == n)
+        def _(n=n):
+            whole = plane_rows.at[pl.ds(1, squares - 1 - n)]
+            remote(whole, whole, plane_send, plane_recv, here).wait_send()
+
+    for target, mine in zip(targets, chosen):
+
+        @pl.when(jnp.logical_not(mine))
+        def _(target=target):
+            copy_to(target).wait_send()
 
 
 def deliver(sol_v, res_v, sol_h, res_h, sem):
@@ -585,7 +669,13 @@
                 dma((2,)),
             ]
             + [dma] * 12
-            + [pltpu.SemaphoreType.REGULAR] * 2,
+            + [pltpu.SemaphoreType.REGULAR] * 2
+            + [
+                pltpu.VMEM((sizes[0] * sizes[1] * sizes[2], 1, 128), F32),
+                pltpu.VMEM((1, 128), F32),
+                dma((1,)),
+                dma((1,)),
+            ],
             compiler_params=pltpu.CompilerParams(collective_id=0, has_side_effects=True),
         )(*operands)
         sol, res = pl.pallas_call(

time: 43.8 us -> 41.9 us (0.957)
  Pallas kernels: 43 us -> 41.1 us
    pallas_call x1, Pallas kernels: 42.4 us -> 40.4 us  [shards(): pl.pallas_call(functools.partial(kernel, sizes), out_shape=(pltpu.VMEM((2...]
where the time goes in v3:
time: 41.9 us; the launch traced here: 41.7 us
  Pallas kernels  41.1 us (98%)
  between operations  0.64 us (2%)
    pallas_call x1, Pallas kernels, shards(): pl.pallas_call(functools.partial(kernel, sizes), out_shape=(pltpu.VMEM((2...  40.4 us

profile of v3, /device:TPU:1, one launch (start us, length us, event | category | flops | bytes accessed | tf_op | source)
XLA Modules:
  0.0 41.7 jit_solution(17454950789092863993)
XLA Ops:
  0.6 40.4 %shard_map.77 = (f32[24,128]{1,0:T(8,128)S(1)}, f32[24,128]{1,0:T(8,128)S(1)}) custom-call(f32[24,128]{1,0:T(8,128)} %bitcast.15, f32[144,128]{1,0:T(8,128)} %bitcast.14, bf16[576,128]{1,0:T(8,128)(2,1)} %bitcast.12, f32[2592,128]{1,0:T(8,128)} %bitcast.10, f32[288,128]{1,0:T(8,128)} %bitcast.13, f32[756,1,128]{2,1,0:T(1,128)} %bitcast.11), custom_call_target="tpu_custom_call" | custom-call | tf_op jit(solution)/shard_map/pallas_call | solution.py:642
  41.1 0.6 %shard_map.78 = (f32[24,128]{1,0:T(8,128)}, f32[24,128]{1,0:T(8,128)}) custom-call(f32[24,128]{1,0:T(8,128)S(1)} %get-tuple-element.6.sol_v, f32[24,128]{1,0:T(8,128)S(1)} %get-tuple-element.7.res_v), custom_call_target="tpu_custom_call" | custom-call | tf_op jit(solution)/shard_map/pallas_call | solution.py:681

commit v4 on v3

--- a/solution.py
+++ b/solution.py
@@ -40,21 +40,6 @@
             plane[(dt, dz, 0)] = len(plane)
     line = {(0, 0, dx): dx for dx in range(sizes[2])}
     return wrapped, slots, plane, line
-
-
-def pieces(value):
-    high = value.astype(BF16)
-    rest = value - high.astype(F32)
-    middle = rest.astype(BF16)
-    low = (rest - middle.astype(F32)).astype(BF16)
-    return high, middle, low
-
-
-def row_sums(value):
-    ones = jnp.ones((8, 384), BF16)
-    dims = (((1,), (1,)), ((), ()))
-    stacked = jnp.concatenate(pieces(value), axis=1)
-    return lax.dot_general(ones, stacked, dims, preferred_element_type=F32)
 
 
 def lanes_from(value, places):
@@ -108,12 +93,11 @@
             )
         )
     ]
-    for load in loads:
-        load.start()
-
     barrier = pltpu.get_barrier_semaphore()
     for step in STEPS:
         pl.semaphore_signal(barrier, inc=1, device_id=at(step), device_id_type=MESH)
+    for load in loads:
+        load.start()
 
     def is_here(place):
         same = [h == o for h, o in zip(here, place)]
@@ -388,7 +372,12 @@
         q_im = q_im + (vr * mi - vi * mr)
     sum_rows[0:24, :] = q_re
     sum_rows[32:56, :] = q_im
-    right_rows[pl.ds(0, 1), pl.ds(0, 64)] = row_sums(sum_rows[...])[0:1]
+    column = jnp.sum(sum_rows[...], axis=1, keepdims=True)
+    lanes64 = lax.broadcasted_iota(jnp.int32, (64, 128), 1)
+    rows64 = lax.broadcasted_iota(jnp.int32, (64, 128), 0)
+    right_rows[pl.ds(0, 1), :] = jnp.sum(
+        jnp.where(lanes64 == rows64, column, 0.0), axis=0, keepdims=True
+    )
 
     if near_count:
         pl.semaphore_wait(near_token, near_count)
@@ -461,7 +450,7 @@
         t, z, x = (lax.rem(h + n - o, n) for h, o, n in zip(here, target, sizes))
         row = (t * sizes[1] + z) * sizes[2] + x
         return remote(
-            line_rows.at[pl.ds(0, 1)], all_rows.at[pl.ds(row, 1), 0], all_send.at[0], all_recv.at[0], target
+            line_rows.at[pl.ds(0, 1)], all_rows.at[pl.ds(row, 1)], all_send.at[0], all_recv.at[0], target
         )
 
     for target, mine in zip(targets, chosen):
@@ -560,8 +549,8 @@
     def _():
         whole = all_rows.at[pl.ds(1, everyone - 1)]
         remote(whole, whole, all_send.at[0], all_recv.at[0], here).wait_recv()
-        all_rows[pl.ds(0, 1)] = line_rows[pl.ds(0, 1), :].reshape(1, 1, 128)
-        total_row[...] = jnp.sum(all_rows[...].reshape(everyone, 128), axis=0, keepdims=True)
+        all_rows[pl.ds(0, 1), :] = line_rows[pl.ds(0, 1), :]
+        total_row[...] = jnp.sum(all_rows[...], axis=0, keepdims=True)
 
     @pl.when(jnp.logical_not(served))
     def _():
@@ -671,7 +660,7 @@
             + [dma] * 12
             + [pltpu.SemaphoreType.REGULAR] * 2
             + [
-                pltpu.VMEM((sizes[0] * sizes[1] * sizes[2], 1, 128), F32),
+                pltpu.VMEM((sizes[0] * sizes[1] * sizes[2], 128), F32),
                 pltpu.VMEM((1, 128), F32),
                 dma((1,)),
                 dma((1,)),

time: 41.9 us -> 41.7 us (level)
  no operation moved by 1% of the time
where the time goes in v4:
time: 41.7 us; the launch traced here: 41.5 us
  Pallas kernels  40.9 us (98%)
  between operations  0.64 us (2%)
    pallas_call x1, Pallas kernels, shards(): pl.pallas_call(functools.partial(kernel, sizes), out_shape=(pltpu.VMEM((2...  40.3 us

profile of v4, /device:TPU:1, one launch (start us, length us, event | category | flops | bytes accessed | tf_op | source)
XLA Modules:
  0.0 41.5 jit_solution(2994556176336669975)
XLA Ops:
  0.6 40.3 %shard_map.77 = (f32[24,128]{1,0:T(8,128)S(1)}, f32[24,128]{1,0:T(8,128)S(1)}) custom-call(f32[24,128]{1,0:T(8,128)} %bitcast.15, f32[144,128]{1,0:T(8,128)} %bitcast.14, bf16[576,128]{1,0:T(8,128)(2,1)} %bitcast.12, f32[2592,128]{1,0:T(8,128)} %bitcast.10, f32[288,128]{1,0:T(8,128)} %bitcast.13, f32[756,1,128]{2,1,0:T(1,128)} %bitcast.11), custom_call_target="tpu_custom_call" | custom-call | tf_op jit(solution)/shard_map/pallas_call | solution.py:631
  40.9 0.6 %shard_map.78 = (f32[24,128]{1,0:T(8,128)}, f32[24,128]{1,0:T(8,128)}) custom-call(f32[24,128]{1,0:T(8,128)S(1)} %get-tuple-element.6.sol_v, f32[24,128]{1,0:T(8,128)S(1)} %get-tuple-element.7.res_v), custom_call_target="tpu_custom_call" | custom-call | tf_op jit(solution)/shard_map/pallas_call | solution.py:670

commit v5 on v4

--- a/solution.py
+++ b/solution.py
@@ -281,11 +281,12 @@
 
     loads[1].wait()
 
+    link = [
+        [[gauge[pl.ds(p * 72 + c * 3 + e, 8, stride=9), :] for e in range(3)] for c in range(3)]
+        for p in range(2)
+    ]
+
     def hopping(which):
-        link = [
-            [[gauge[pl.ds(p * 72 + c * 3 + e, 8, stride=9), :] for e in range(3)] for c in range(3)]
-            for p in range(2)
-        ]
         half = [
             [[halo[which, :, p * 6 + s * 3 + c, :] for c in range(3)] for s in range(2)]
             for p in range(2)
@@ -334,8 +335,6 @@
     second_copies.arrived()
     hopping(1)
     res_re, res_im = residual(second_re, second_im)
-    res_ref[0:12, :] = res_re
-    res_ref[12:24, :] = res_im
     hop_rows[0:12, :] = res_re.astype(BF16).astype(F32)
     hop_rows[12:24, :] = res_im.astype(BF16).astype(F32)
 
@@ -384,6 +383,8 @@
     right_copies = Group(
         right_rows.at[pl.ds(0, 1)], right_rows, right_send, right_recv, [o for o in slots.items() if o[1]]
     ).start()
+    res_ref[0:12, :] = res_re
+    res_ref[12:24, :] = res_im
     final[pl.ds(96, 48), :] = 0.4 * four_lanes(parts, 4 * (lane_row // 4))
     blk_copies.arrived()
     for d in range(4):

time: 41.7 us -> 41.7 us (level)
  no operation moved by 1% of the time
where the time goes in v5:
time: 41.7 us; the launch traced here: 41.5 us
  Pallas kernels  40.9 us (98%)
  between operations  0.64 us (2%)
    pallas_call x1, Pallas kernels, shards(): pl.pallas_call(functools.partial(kernel, sizes), out_shape=(pltpu.VMEM((2...  40.3 us

profile of v5, /device:TPU:1, one launch (start us, length us, event | category | flops | bytes accessed | tf_op | source)
XLA Modules:
  0.0 41.5 jit_solution(8140622189722690559)
XLA Ops:
  0.6 40.3 %shard_map.77 = (f32[24,128]{1,0:T(8,128)S(1)}, f32[24,128]{1,0:T(8,128)S(1)}) custom-call(f32[24,128]{1,0:T(8,128)} %bitcast.15, f32[144,128]{1,0:T(8,128)} %bitcast.14, bf16[576,128]{1,0:T(8,128)(2,1)} %bitcast.12, f32[2592,128]{1,0:T(8,128)} %bitcast.10, f32[288,128]{1,0:T(8,128)} %bitcast.13, f32[756,1,128]{2,1,0:T(1,128)} %bitcast.11), custom_call_target="tpu_custom_call" | custom-call | tf_op jit(solution)/shard_map/pallas_call | solution.py:632
  40.9 0.6 %shard_map.78 = (f32[24,128]{1,0:T(8,128)}, f32[24,128]{1,0:T(8,128)}) custom-call(f32[24,128]{1,0:T(8,128)S(1)} %get-tuple-element.6.sol_v, f32[24,128]{1,0:T(8,128)S(1)} %get-tuple-element.7.res_v), custom_call_target="tpu_custom_call" | custom-call | tf_op jit(solution)/shard_map/pallas_call | solution.py:671
